TPU v7x, 32 devices: a whole 2x2x4 slice. The times are simulated.
32 devices in a mesh: groups: 2 (over y), dp: 4 (over z), mp: 4 (over x, core).
Axes of the slice: x: 2, y: 2, z: 4, core: 2. Of those that a mesh axis runs over, the one named last changes fastest.
Arguments:
- hidden: bfloat16 [8, 8192], P(('groups', 'mp'), 'dp'), parts along dimension 0, may hold values from -530 to 530
- attention_gain: float32 [8192], P('dp'), may hold values from 0.25 to 1.75
- query_weight: bfloat16 [8192, 8192], P('dp', 'mp'), may hold values from -0.0625 to 0.0625
- key_projector: bfloat16 [8192, 1024], P('dp', 'mp'), may hold values from -0.0625 to 0.0625
- value_projector: bfloat16 [8192, 1024], P('dp', 'mp'), may hold values from -0.0625 to 0.0625
- out_weight: bfloat16 [8192, 8192], P('mp', 'dp'), may hold values from -0.1875 to 0.1875
- key_cache: bfloat16 [8, 8, 256, 128], P(('groups', 'dp'), 'mp'), parts along dimension 0, may hold values from -1230 to 1230
- earlier_value_cache: bfloat16 [8, 8, 256, 128], P(('groups', 'dp'), 'mp'), parts along dimension 0, may hold values from -6 to 6
- cached_length_per_row: int32 [8], P(('groups', 'dp')), parts along dimension 0, may hold values from 1 to 256
- final_gain: float32 [8192], replicated, may hold values from 0.25 to 1.75
- head_weight: bfloat16 [32000, 8192], P('dp', 'mp'), may hold values from -41 to 41
- draft_ids: int32 [8], P(('groups', 'mp')), parts along dimension 0, may hold values from 0 to 31999
Outputs:
- residual_out: bfloat16 [8, 8192], P(('groups', 'mp'), 'dp'), parts along dimension 0
- draft_logprob: float32 [8], P(('groups', 'mp')), parts along dimension 0
There are 2 independent parts, one for each index of `groups`. A program takes and returns all parts, laid end to end along the dimension named above; an argument that names none is the same for every part. Nothing has to cross between parts.
All inputs are finite; a program needn't handle non-finite values.
Results may differ from a plain program's by a relative error of at most 0.0035.
Values may be sent and summed in bfloat16 or wider, within the bound.
A program may use at most 128 MiB of HBM per device.

v0:
```python
import jax
import jax.numpy as jnp
from jax import lax
from jax.sharding import PartitionSpec as P

MODEL_WIDTH = 8192
EPSILON = 1e-05
THETA = 10000.0


def rotary_embedding(vectors, positions):
    half_dim = vectors.shape[-1] // 2
    frequency = THETA ** (-2.0 * jnp.arange(half_dim, dtype=jnp.float32) / vectors.shape[-1])
    angles = positions.astype(jnp.float32)[:, None, None] * frequency[None, None, :]
    cosine = jnp.cos(angles)
    sine_part = jnp.sin(angles)
    former = vectors[..., :half_dim]
    latter = vectors[..., half_dim:]
    return jnp.concatenate(
        [former * cosine - latter * sine_part, latter * cosine + former * sine_part], axis=-1
    )


def rms_normed(matrix, gain_row):
    wide_rows = matrix.astype(jnp.float32)
    mean_square = jnp.mean(wide_rows * wide_rows, axis=-1, keepdims=True)
    return (wide_rows * lax.rsqrt(mean_square + EPSILON) * gain_row).astype(jnp.bfloat16)


def shards(
    hidden,
    attention_gain,
    query_weight,
    key_projector,
    value_projector,
    out_weight,
    key_cache,
    earlier_value_cache,
    cached_length_per_row,
    final_gain,
    head_weight,
    draft_ids,
):
    sequences = key_cache.shape[0]
    local_pairs = key_cache.shape[1]
    head_size = key_cache.shape[3]
    query_cols = query_weight.shape[1]
    pair_cols = key_projector.shape[1]
    local_heads = query_cols // head_size
    group_size = local_heads // local_pairs
    hidden_wide = hidden.astype(jnp.float32)
    squares_in = lax.psum(jnp.sum(hidden_wide * hidden_wide, axis=1), "dp")
    normed = (
        hidden_wide * lax.rsqrt(squares_in / MODEL_WIDTH + EPSILON)[:, None] * attention_gain
    ).astype(jnp.bfloat16)
    all_rows = lax.all_gather(normed, "mp", axis=0, tiled=True)
    picked_rows = all_rows
    projected = lax.psum_scatter(
        jnp.concatenate(
            [
                jnp.dot(picked_rows, weight, preferred_element_type=jnp.float32)
                for weight in (query_weight, key_projector, value_projector)
            ],
            axis=1,
        ),
        "dp",
        scatter_dimension=0,
        tiled=True,
    )
    query_rows = rotary_embedding(
        projected[:, :query_cols].reshape(sequences, local_heads, head_size), cached_length_per_row
    ).astype(jnp.bfloat16)
    query_rows = query_rows.reshape(sequences, local_pairs, group_size, head_size)
    incoming_key = rotary_embedding(
        projected[:, query_cols : query_cols + pair_cols].reshape(
            sequences, local_pairs, head_size
        ),
        cached_length_per_row,
    ).astype(jnp.bfloat16)
    incoming_value = (
        projected[:, query_cols + pair_cols :]
        .reshape(sequences, local_pairs, head_size)
        .astype(jnp.bfloat16)
    )
    score_scale = head_size ** (-0.5)
    own_score = (
        jnp.einsum("bgrd,bgd->bgr", query_rows, incoming_key, preferred_element_type=jnp.float32)
        * score_scale
    )
    scores = (
        jnp.einsum("bgrd,bgtd->bgrt", query_rows, key_cache, preferred_element_type=jnp.float32)
        * score_scale
    )
    places = lax.broadcasted_iota(jnp.int32, scores.shape, 3)
    scores = jnp.where(places < cached_length_per_row[:, None, None, None], scores, -jnp.inf)
    highest = jnp.maximum(jnp.max(scores, axis=3), own_score)
    exponent = jnp.exp(scores - highest[..., None])
    denominator = jnp.sum(exponent, axis=3)
    numerator = jnp.einsum(
        "bgrt,bgtd->bgrd",
        exponent.astype(jnp.bfloat16),
        earlier_value_cache,
        preferred_element_type=jnp.float32,
    )
    own_exp = jnp.exp(own_score - highest)
    denominator = denominator + own_exp
    own_weight = lax.optimization_barrier(own_exp.astype(jnp.bfloat16)).astype(jnp.float32)
    numerator = (
        numerator + own_weight[..., None] * incoming_value.astype(jnp.float32)[:, :, None, :]
    )
    mixed_heads = (
        (numerator / denominator[..., None]).astype(jnp.bfloat16).reshape(sequences, query_cols)
    )
    gathered = lax.all_gather(mixed_heads, "dp", axis=0, tiled=True)
    picked_rows = gathered
    attention_out = lax.psum_scatter(
        jnp.dot(picked_rows, out_weight, preferred_element_type=jnp.float32),
        "mp",
        scatter_dimension=0,
        tiled=True,
    )
    residual_out = (hidden_wide + attention_out).astype(jnp.bfloat16)
    full_rows = lax.all_gather(residual_out, "dp", axis=1, tiled=True)
    full_rows = rms_normed(full_rows, final_gain)
    columns = lax.all_to_all(full_rows, "mp", split_axis=1, concat_axis=0, tiled=True)
    picked_rows = columns
    logits = lax.psum_scatter(
        jnp.einsum("bd,vd->bv", picked_rows, head_weight, preferred_element_type=jnp.float32),
        "mp",
        scatter_dimension=0,
        tiled=True,
    )
    vocab_first = lax.axis_index("dp") * head_weight.shape[0]
    local_peak = jnp.max(logits, axis=1)
    local_mass = jnp.sum(jnp.exp(logits - local_peak[:, None]), axis=1)
    matches = lax.broadcasted_iota(jnp.int32, logits.shape, 1) + vocab_first == draft_ids[:, None]
    target_logit = jnp.sum(jnp.where(matches, logits, 0.0), axis=1)
    overall_peak = lax.pmax(local_peak, "dp")
    total_mass, total_target = lax.psum(
        (local_mass * jnp.exp(local_peak - overall_peak), target_logit), "dp"
    )
    log_total = overall_peak + jnp.log(total_mass)
    return (residual_out, total_target - log_total)


def solution(mesh):
    in_specs = (
        P(("groups", "mp"), "dp"),
        P("dp"),
        P("dp", "mp"),
        P("dp", "mp"),
        P("dp", "mp"),
        P("mp", "dp"),
        P(("groups", "dp"), "mp", None, None),
        P(("groups", "dp"), "mp", None, None),
        P(("groups", "dp")),
        P(),
        P("dp", "mp"),
        P(("groups", "mp")),
    )
    out_specs = (P(("groups", "mp"), "dp"), P(("groups", "mp")))
    return jax.shard_map(shards, mesh=mesh, in_specs=in_specs, out_specs=out_specs, check_vma=False)
```

profile of v0, /device:TPU:0, one launch (start us, length us, event | category | flops | bytes accessed | tf_op | source)
XLA Modules:
  0.0 190.5 jit_solution(16684031391719572066)
XLA Ops:
  7.2 0.0 copy-start
  7.2 0.0 all-reduce.6.cloned.1.call-start
  7.2 1.4 multiply_reduce_fusion.1
  8.6 14.1 %psum.21 = f32[1]{0:T(128)} all-reduce(f32[1]{0:T(128)} %bitcast.1), channel_id=1, replica_groups=mesh['groups'=2,'dp'=4,'mp'=4] {'dp'}, use_global_device_ids=true, to_apply=%region_1.0 | all-reduce | flops 1 | bytes 8 | tf_op jit(solution)/shard_map/psum | solution.py:52
  23.4 0.7 convert_bitcast_fusion
  24.1 5.2 %all-gather = bf16[4,1,2048]{2,1,0:T(2,128)(2,1)S(1)} all-gather(bf16[1,1,2048]{2,1,0:T(2,128)(2,1)S(1)} %convert_bitcast_fusion), channel_id=1, replica_groups=mesh['groups'=2,'dp'=4,'mp'=4] {'mp'}, dimensions={0}, use_global_device_ids=true | all-gather | bytes 20480 | tf_op jit(solution)/shard_map/all_gather | solution.py:56
  29.3 0.0 copy-start.1
  29.3 0.0 copy-start.8
  29.3 0.0 copy-start.2
  29.3 0.0 copy-start.6
  29.3 4.7 %fusion.16 = f32[4,2048]{1,0:T(4,128)S(1)} fusion(bf16[2048,2048]{1,0:T(8,128)(2,1)} %param.14, bf16[4,1,2048]{2,1,0:T(2,128)(2,1)S(1)} %all-gather), kind=kOutput, calls=%fused_computation.23 | convolution fusion | flops 33554432 | bytes 8437760 | tf_op jit(solution)/shard_map/dot_general | solution.py:61
  34.0 0.0 copy-done
  34.0 0.2 fusion.12
  34.3 0.0 copy-done.1
  34.3 0.3 fusion.14
  34.5 0.0 copy-start.7
  34.5 0.0 copy-start.3
  34.5 0.0 copy-start.4
  34.6 16.2 %all-reduce = f32[4,2560]{1,0:T(4,128)S(1)} all-reduce(f32[4,2560]{1,0:T(4,128)S(1)} %pad_maximum_fusion), channel_id=2, replica_groups=mesh['groups'=2,'dp'=4,'mp'=4] {'dp'}, use_global_device_ids=true, to_apply=%region_2.0.clone | all-reduce | flops 10240 | bytes 81920
  50.8 0.0 copy-done.8
  50.8 0.6 dynamic-slice
  51.4 0.7 constant_dynamic-slice_fusion
  52.1 0.7 dynamic-slice.7
  53.5 0.1 fusion.28
  53.6 0.1 fusion.23
  53.6 0.1 maximum_bitcast_fusion
  53.7 0.2 fusion.26
  53.9 0.0 copy-done.2
  53.9 0.3 fusion.38
  54.2 0.2 fusion.18
  54.4 0.7 fusion.25
  55.1 0.0 copy-done.6
  55.1 0.2 fusion.2
  55.3 13.1 %all-gather.1 = bf16[4,1,2048]{2,1,0:T(2,128)(2,1)S(1)} all-gather(bf16[1,1,2048]{2,1,0:T(2,128)(2,1)S(1)} %reshape.192), channel_id=1, replica_groups=mesh['groups'=2,'dp'=4,'mp'=4] {'dp'}, dimensions={0}, use_global_device_ids=true | all-gather | bytes 20480 | tf_op jit(solution)/shard_map/all_gather | solution.py:114
  68.5 4.6 %fusion.9 = f32[4,2048]{1,0:T(4,128)S(1)} fusion(bf16[2048,2048]{1,0:T(8,128)(2,1)} %param.17, bf16[4,1,2048]{2,1,0:T(2,128)(2,1)S(1)} %all-gather.1), kind=kOutput, calls=%fused_computation.16 | convolution fusion | flops 33554432 | bytes 8437760 | tf_op jit(solution)/shard_map/dot_general | solution.py:117
  73.0 10.3 %all-reduce.1 = f32[4,2048]{1,0:T(4,128)S(1)} all-reduce(f32[4,2048]{1,0:T(4,128)S(1)} %fusion.9), channel_id=3, replica_groups=mesh['groups'=2,'dp'=4,'mp'=4] {'mp'}, use_global_device_ids=true, to_apply=%region_5.6.clone | all-reduce | flops 8192 | bytes 65536
  83.3 0.0 copy-done.7
  83.3 0.6 dynamic-slice.2
  83.9 0.0 copy-done.3
  83.9 0.7 fusion.21
  84.6 0.0 copy-start.5
  84.6 13.1 %all_gather.11 = bf16[1,8192]{1,0:T(2,128)(2,1)S(1)} all-gather(bf16[1,2048]{1,0:T(2,128)(2,1)S(1)} %fusion.21), channel_id=1, replica_groups=mesh['groups'=2,'dp'=4,'mp'=4] {'dp'}, dimensions={1}, use_global_device_ids=true | all-gather | bytes 20480 | tf_op jit(solution)/shard_map/all_gather | solution.py:123
  97.7 0.7 multiply_reduce_fusion
  99.2 0.0 copy-done.4
  99.2 0.1 multiply_convert_fusion
  99.3 0.6 broadcast.94
  99.9 0.8 reduce.9
  100.7 6.6 %all_to_all.16 = bf16[4,2,1024]{2,1,0:T(2,128)(2,1)S(1)} all-to-all(bf16[4,2,1024]{2,1,0:T(2,128)(2,1)S(1)} %reshape.200), channel_id=1, replica_groups=mesh['groups'=2,'dp'=4,'mp'=4] {'mp'}, dimensions={0} | all-to-all | bytes 32768 | tf_op jit(solution)/shard_map/all_to_all | solution.py:125
  107.3 14.4 %fusion.6 = f32[4,8000]{1,0:T(4,128)} fusion(bf16[8000,2048]{1,0:T(8,128)(2,1)} %param.22, bf16[1,4,2048]{2,0,1:T(2,128)(2,1)S(1)} %bitcast.66), kind=kOutput, calls=%fused_computation.13 | convolution fusion | flops 131072000 | bytes 32912384 | tf_op jit(solution)/shard_map/bd,vd->bv/dot_general | solution.py:128
  121.6 0.0 copy-done.5
  121.6 0.0 all-reduce.6.cloned.1.call-update
  122.3 29.9 %all-reduce.6.cloned.1.call-done = f32[4,8000]{1,0:T(4,128)} async-done(((f32[4,8000]{1,0:T(4,128)}), f32[4,8000]{1,0:T(4,128)}) %all-reduce.6.cloned.1.call-update) | async-done | bytes 128016
  152.2 2.3 %dynamic-slice_reduce_fusion = f32[]{:T(128)} fusion(f32[4,8000]{1,0:T(4,128)} %all-reduce.6.cloned.1.call-done, u32[]{:T(128)} %bitcast.28), kind=kLoop, calls=%fused_computation.39 | loop fusion | flops 7999 | bytes 32008 | tf_op jit(solution)/shard_map/reduce_max | solution.py:134
  154.5 12.3 %pmax.7 = f32[1]{0:T(128)} all-reduce(f32[1]{0:T(128)} %bitcast.24), channel_id=1, replica_groups=mesh['groups'=2,'dp'=4,'mp'=4] {'dp'}, use_global_device_ids=true, to_apply=%region_11.12 | all-reduce | flops 1 | bytes 8 | tf_op jit(solution)/shard_map/pmax | solution.py:138
  168.0 3.0 %exponential_reduce_fusion = (f32[]{:T(128)}, f32[]{:T(128)}) fusion(f32[]{:T(128)} %dynamic-slice_reduce_fusion, f32[4,8000]{1,0:T(4,128)} %all-reduce.6.cloned.1.call-done, u32[]{:T(128)} %bitcast.28, s32[]{:T(128)} %bitcast.64, s32[]{:T(128)S(6)} %mul.175), kind=kLoop, calls=%fused_computation.11 | loop fusion | flops 47998 | bytes 32024 | tf_op jit(solution)/shard_map/reduce_sum | solution.py:135
  171.7 8.9 %all-reduce.3 = (f32[1]{0:T(128)}, f32[1]{0:T(128)}) all-reduce(f32[1]{0:T(128)} %bitcast.23, f32[1]{0:T(128)S(6)} %mul.180), channel_id=1, replica_groups=mesh['groups'=2,'dp'=4,'mp'=4] {'dp'}, use_global_device_ids=true, to_apply=%region_9.10 | all-reduce | flops 2 | bytes 16 | tf_op jit(solution)/shard_map/psum | solution.py:139
  (8 shorter events, 0.1 us)
Async XLA Ops:
  7.2 26.9 %copy-start = (bf16[2048,256]{1,0:T(8,128)(2,1)S(1)}, bf16[2048,256]{1,0:T(8,128)(2,1)}, u32[]{:S(2)}) copy-start(bf16[2048,256]{1,0:T(8,128)(2,1)} %param.16) | copy-start | bytes 3145732
  7.2 145.0 %all-reduce.6.cloned.1.call-start = ((), (), s32[]{:S(2)}) async-start(), calls=%async_computation.1 | async-start | bytes 258048
  29.3 4.9 %copy-start.1 = (bf16[2048,256]{1,0:T(8,128)(2,1)S(1)}, bf16[2048,256]{1,0:T(8,128)(2,1)}, u32[]{:S(2)}) copy-start(bf16[2048,256]{1,0:T(8,128)(2,1)} %param.15) | copy-start | bytes 3145732
  29.3 21.5 %copy-start.8 = (u32[32]{0:T(128)S(1)}, u32[32]{0:T(128)}, u32[]{:S(2)}) copy-start(u32[32]{0:T(128)} %constant.41) | copy-start | bytes 388
  29.3 24.6 %copy-start.2 = (bf16[1,2,256,128]{3,2,1,0:T(8,128)(2,1)S(1)}, bf16[1,2,256,128]{3,2,1,0:T(8,128)(2,1)}, u32[]{:S(2)}) copy-start(bf16[1,2,256,128]{3,2,1,0:T(8,128)(2,1)} %param.18) | copy-start | bytes 393220
  29.3 25.8 %copy-start.6 = (bf16[1,2,256,128]{3,2,1,0:T(8,128)(2,1)S(1)}, bf16[1,2,256,128]{3,2,1,0:T(8,128)(2,1)}, u32[]{:S(2)}) copy-start(bf16[1,2,256,128]{3,2,1,0:T(8,128)(2,1)} %param.19) | copy-start | bytes 393220
  34.5 48.8 %copy-start.7 = (u32[32]{0:T(128)S(1)}, u32[32]{0:T(128)}, u32[]{:S(2)}) copy-start(u32[32]{0:T(128)} %constant.45) | copy-start | bytes 388
  34.5 49.4 %copy-start.3 = (bf16[1,2048]{1,0:T(2,128)(2,1)S(1)}, bf16[1,2048]{1,0:T(2,128)(2,1)}, u32[]{:S(2)}) copy-start(bf16[1,2048]{1,0:T(2,128)(2,1)} %param.12) | copy-start | bytes 12292
  34.5 64.7 %copy-start.4 = (f32[8192]{0:T(1024)S(1)}, f32[8192]{0:T(1024)}, u32[]{:S(2)}) copy-start(f32[8192]{0:T(1024)} %param.21) | copy-start | bytes 98308
  84.6 37.0 %copy-start.5 = (bf16[1,2048]{1,0:T(2,128)(2,1)}, bf16[1,2048]{1,0:T(2,128)(2,1)S(1)}, u32[]{:S(2)}) copy-start(bf16[1,2048]{1,0:T(2,128)(2,1)S(1)} %fusion.21) | copy-start | bytes 12292
Sparse Core Ops, SparseCore 0:
  121.8 30.3 all-reduce.5
where the time goes:
time: 191 us
  blocking collectives  99.8 us (52%)
  waiting for transfers between devices  29.9 us (16%)
  matrix products  24.8 us (13%)
  between operations  21.9 us (11%)
  other arithmetic  10.9 us (6%)
  local copies, waits for them, and re-layouts  3.24 us (2%)
    unnamed x2, waiting for transfers between devices  29.9 us
    unnamed x2, blocking collectives  26.5 us
    dot_general x1, matrix products, shards(): jnp.einsum('bd,vd->bv', picked_rows, head_weight, preferred_element_type=...  14.4 us
    psum x1, blocking collectives, shards(): squares_in = lax.psum(jnp.sum(hidden_wide * hidden_wide, axis=1), 'dp')  14.1 us
    all_gather x1, blocking collectives, shards(): full_rows = lax.all_gather(residual_out, 'dp', axis=1, tiled=True)  13.1 us
    all_gather x1, blocking collectives, shards(): gathered = lax.all_gather(mixed_heads, 'dp', axis=0, tiled=True)  13.1 us
    pmax x1, blocking collectives, shards(): overall_peak = lax.pmax(local_peak, 'dp')  12.3 us
    psum x1, blocking collectives, shards(): lax.psum((local_mass * jnp.exp(local_peak - overall_peak), target_logit),...  8.95 us
  transfers between devices with their start and end apart: 1, of which 1 were waited for; matrix products, arithmetic and copies ran while one was open for 0% of the time, Pallas kernels for 0%

commit v1 on v0

--- a/solution.py
+++ b/solution.py
@@ -6,6 +6,16 @@
 MODEL_WIDTH = 8192
 EPSILON = 1e-05
 THETA = 10000.0
+
+
+def pass_along(shard, axis, dim):
+    size = lax.axis_size(axis)
+    held, blocks = (shard, [shard])
+    for _ in range(size - 1):
+        held = lax.ppermute(held, axis, [(i, (i + 1) % size) for i in range(size)])
+        blocks.insert(0, held)
+    flat = jnp.concatenate(blocks, axis=dim)
+    return jnp.roll(flat, (lax.axis_index(axis) + 1) * shard.shape[dim], axis=dim)
 
 
 def rotary_embedding(vectors, positions):
@@ -120,7 +130,7 @@
         tiled=True,
     )
     residual_out = (hidden_wide + attention_out).astype(jnp.bfloat16)
-    full_rows = lax.all_gather(residual_out, "dp", axis=1, tiled=True)
+    full_rows = pass_along(residual_out, "dp", 1)
     full_rows = rms_normed(full_rows, final_gain)
     columns = lax.all_to_all(full_rows, "mp", split_axis=1, concat_axis=0, tiled=True)
     picked_rows = columns

time: 191 us -> 193 us (1.010)
  waiting for transfers between devices: 29.9 us -> 44.7 us
  blocking collectives: 99.8 us -> 86.7 us
    ppermute x0 -> x3, waiting for transfers between devices: none -> 16.2 us  [pass_along(): held = lax.ppermute(held, axis, [(i, (i + 1) % size) for i in range(size)])]
    all_gather x1 -> x0, blocking collectives: 13.1 us -> none  [shards(): full_rows = lax.all_gather(residual_out, 'dp', axis=1, tiled=True)]
  transfers between devices with their start and end apart: 1 -> 4, of which waited for: 1 -> 4; matrix products, arithmetic and copies ran while one was open for 0% -> 0% of each run, Pallas kernels for 0% -> 0%
where the time goes in v1:
time: 193 us
  blocking collectives  86.7 us (45%)
  waiting for transfers between devices  44.7 us (23%)
  matrix products  24.8 us (13%)
  between operations  22 us (11%)
  other arithmetic  10.9 us (6%)
  local copies, waits for them, and re-layouts  3.36 us (2%)
    unnamed x2, waiting for transfers between devices  28.5 us
    unnamed x2, blocking collectives  26.5 us
    ppermute x3, waiting for transfers between devices, pass_along(): held = lax.ppermute(held, axis, [(i, (i + 1) % size) for i in range(size)])  16.2 us
    dot_general x1, matrix products, shards(): jnp.einsum('bd,vd->bv', picked_rows, head_weight, preferred_element_type=...  14.4 us
    psum x1, blocking collectives, shards(): squares_in = lax.psum(jnp.sum(hidden_wide * hidden_wide, axis=1), 'dp')  14.1 us
    all_gather x1, blocking collectives, shards(): gathered = lax.all_gather(mixed_heads, 'dp', axis=0, tiled=True)  13.1 us
    pmax x1, blocking collectives, shards(): overall_peak = lax.pmax(local_peak, 'dp')  12.3 us
    psum x1, blocking collectives, shards(): lax.psum((local_mass * jnp.exp(local_peak - overall_peak), target_logit),...  8.95 us
  transfers between devices with their start and end apart: 4, of which 4 were waited for; matrix products, arithmetic and copies ran while one was open for 0% of the time, Pallas kernels for 0%

profile of v1, /device:TPU:0, one launch (start us, length us, event | category | flops | bytes accessed | tf_op | source)
XLA Modules:
  0.0 192.6 jit_solution(1920496729438574153)
XLA Ops:
  7.2 0.0 copy-start
  7.2 0.0 all-reduce.6.cloned.1.call-start
  7.2 1.4 multiply_reduce_fusion.1
  8.6 14.1 %psum.21 = f32[1]{0:T(128)} all-reduce(f32[1]{0:T(128)} %bitcast.1), channel_id=1, replica_groups=mesh['groups'=2,'dp'=4,'mp'=4] {'dp'}, use_global_device_ids=true, to_apply=%region_1.0 | all-reduce | flops 1 | bytes 8 | tf_op jit(solution)/shard_map/psum | solution.py:62
  23.4 0.7 convert_bitcast_fusion
  24.1 5.2 %all-gather = bf16[4,1,2048]{2,1,0:T(2,128)(2,1)S(1)} all-gather(bf16[1,1,2048]{2,1,0:T(2,128)(2,1)S(1)} %convert_bitcast_fusion), channel_id=1, replica_groups=mesh['groups'=2,'dp'=4,'mp'=4] {'mp'}, dimensions={0}, use_global_device_ids=true | all-gather | bytes 20480 | tf_op jit(solution)/shard_map/all_gather | solution.py:66
  29.3 0.0 copy-start.1
  29.3 0.0 copy-start.8
  29.3 0.0 copy-start.2
  29.3 0.0 copy-start.6
  29.3 4.7 %fusion.16 = f32[4,2048]{1,0:T(4,128)S(1)} fusion(bf16[2048,2048]{1,0:T(8,128)(2,1)} %param.14, bf16[4,1,2048]{2,1,0:T(2,128)(2,1)S(1)} %all-gather), kind=kOutput, calls=%fused_computation.31 | convolution fusion | flops 33554432 | bytes 8437760 | tf_op jit(solution)/shard_map/dot_general | solution.py:71
  34.0 0.0 copy-done
  34.0 0.2 fusion.12
  34.3 0.0 copy-done.1
  34.3 0.3 fusion.14
  34.5 0.0 copy-start.7
  34.5 0.0 copy-start.3
  34.5 0.0 copy-start.5
  34.6 16.2 %all-reduce = f32[4,2560]{1,0:T(4,128)S(1)} all-reduce(f32[4,2560]{1,0:T(4,128)S(1)} %pad_maximum_fusion), channel_id=2, replica_groups=mesh['groups'=2,'dp'=4,'mp'=4] {'dp'}, use_global_device_ids=true, to_apply=%region_2.0.clone | all-reduce | flops 10240 | bytes 81920
  50.8 0.0 copy-done.8
  50.8 0.6 dynamic-slice
  51.4 0.7 constant_dynamic-slice_fusion
  52.1 0.7 dynamic-slice.7
  53.5 0.1 fusion.28
  53.6 0.1 fusion.23
  53.6 0.1 maximum_bitcast_fusion
  53.7 0.2 fusion.26
  53.9 0.0 copy-done.2
  53.9 0.3 fusion.38
  54.2 0.2 fusion.18
  54.4 0.7 fusion.25
  55.1 0.0 copy-done.6
  55.1 0.2 fusion.2
  55.3 13.1 %all-gather.1 = bf16[4,1,2048]{2,1,0:T(2,128)(2,1)S(1)} all-gather(bf16[1,1,2048]{2,1,0:T(2,128)(2,1)S(1)} %reshape.192), channel_id=1, replica_groups=mesh['groups'=2,'dp'=4,'mp'=4] {'dp'}, dimensions={0}, use_global_device_ids=true | all-gather | bytes 20480 | tf_op jit(solution)/shard_map/all_gather | solution.py:124
  68.5 4.6 %fusion.9 = f32[4,2048]{1,0:T(4,128)S(1)} fusion(bf16[2048,2048]{1,0:T(8,128)(2,1)} %param.17, bf16[4,1,2048]{2,1,0:T(2,128)(2,1)S(1)} %all-gather.1), kind=kOutput, calls=%fused_computation.24 | convolution fusion | flops 33554432 | bytes 8437760 | tf_op jit(solution)/shard_map/dot_general | solution.py:127
  73.0 10.3 %all-reduce.1 = f32[4,2048]{1,0:T(4,128)S(1)} all-reduce(f32[4,2048]{1,0:T(4,128)S(1)} %fusion.9), channel_id=3, replica_groups=mesh['groups'=2,'dp'=4,'mp'=4] {'mp'}, use_global_device_ids=true, to_apply=%region_5.6.clone | all-reduce | flops 8192 | bytes 65536
  83.3 0.0 copy-done.7
  83.3 0.6 dynamic-slice.2
  83.9 0.0 copy-done.3
  83.9 0.7 fusion.21
  84.6 0.0 copy-start.4
  84.6 0.2 collective-permute-start
  84.8 5.3 %collective-permute-done = bf16[1,2048]{1,0:T(2,128)(2,1)S(1)} collective-permute-done((bf16[1,2048]{1,0:T(2,128)(2,1)S(1)}, bf16[1,2048]{1,0:T(2,128)(2,1)S(1)}, u32[]{:S(2)}, u32[]{:S(2)}) %collective-permute-start) | collective-permute-done | bytes 4128 | tf_op jit(solution)/shard_map/ppermute | solution.py:15
  90.1 0.0 collective-permute-start.1
  90.1 5.4 %collective-permute-done.1 = bf16[1,2048]{1,0:T(2,128)(2,1)S(1)} collective-permute-done((bf16[1,2048]{1,0:T(2,128)(2,1)S(1)}, bf16[1,2048]{1,0:T(2,128)(2,1)S(1)}, u32[]{:S(2)}, u32[]{:S(2)}) %collective-permute-start.1) | collective-permute-done | bytes 4128 | tf_op jit(solution)/shard_map/ppermute | solution.py:15
  95.5 0.0 collective-permute-start.2
  95.5 5.4 %collective-permute-done.2 = bf16[1,2048]{1,0:T(2,128)(2,1)S(1)} collective-permute-done((bf16[1,2048]{1,0:T(2,128)(2,1)S(1)}, bf16[1,2048]{1,0:T(2,128)(2,1)S(1)}, u32[]{:S(2)}, u32[]{:S(2)}) %collective-permute-start.2) | collective-permute-done | bytes 4128 | tf_op jit(solution)/shard_map/ppermute | solution.py:15
  101.2 0.8 multiply_reduce_fusion
  102.6 0.0 copy-done.5
  102.7 0.6 broadcast.95
  103.3 0.8 reduce.9
  104.1 6.6 %all_to_all.16 = bf16[4,2,1024]{2,1,0:T(2,128)(2,1)S(1)} all-to-all(bf16[4,2,1024]{2,1,0:T(2,128)(2,1)S(1)} %reshape.200), channel_id=1, replica_groups=mesh['groups'=2,'dp'=4,'mp'=4] {'mp'}, dimensions={0} | all-to-all | bytes 32768 | tf_op jit(solution)/shard_map/all_to_all | solution.py:135
  110.7 14.4 %fusion.6 = f32[4,8000]{1,0:T(4,128)} fusion(bf16[8000,2048]{1,0:T(8,128)(2,1)} %param.22, bf16[1,4,2048]{2,0,1:T(2,128)(2,1)S(1)} %bitcast.66), kind=kOutput, calls=%fused_computation.21 | convolution fusion | flops 131072000 | bytes 32912384 | tf_op jit(solution)/shard_map/bd,vd->bv/dot_general | solution.py:138
  125.1 0.0 copy-done.4
  125.1 0.0 all-reduce.6.cloned.1.call-update
  125.7 28.5 %all-reduce.6.cloned.1.call-done = f32[4,8000]{1,0:T(4,128)} async-done(((f32[4,8000]{1,0:T(4,128)}), f32[4,8000]{1,0:T(4,128)}) %all-reduce.6.cloned.1.call-update) | async-done | bytes 128016
  154.2 2.3 %dynamic-slice_reduce_fusion = f32[]{:T(128)} fusion(f32[4,8000]{1,0:T(4,128)} %all-reduce.6.cloned.1.call-done, u32[]{:T(128)} %bitcast.28), kind=kLoop, calls=%fused_computation.47 | loop fusion | flops 7999 | bytes 32008 | tf_op jit(solution)/shard_map/reduce_max | solution.py:144
  156.5 12.3 %pmax.7 = f32[1]{0:T(128)} all-reduce(f32[1]{0:T(128)} %bitcast.24), channel_id=1, replica_groups=mesh['groups'=2,'dp'=4,'mp'=4] {'dp'}, use_global_device_ids=true, to_apply=%region_11.12 | all-reduce | flops 1 | bytes 8 | tf_op jit(solution)/shard_map/pmax | solution.py:148
  170.1 3.0 %exponential_reduce_fusion = (f32[]{:T(128)}, f32[]{:T(128)}) fusion(f32[]{:T(128)} %dynamic-slice_reduce_fusion, f32[4,8000]{1,0:T(4,128)} %all-reduce.6.cloned.1.call-done, u32[]{:T(128)} %bitcast.28, s32[]{:T(128)} %bitcast.64, s32[]{:T(128)S(6)} %mul.178), kind=kLoop, calls=%fused_computation.11 | loop fusion | flops 47998 | bytes 32024 | tf_op jit(solution)/shard_map/reduce_sum | solution.py:145
  173.7 8.9 %all-reduce.3 = (f32[1]{0:T(128)}, f32[1]{0:T(128)}) all-reduce(f32[1]{0:T(128)} %bitcast.23, f32[1]{0:T(128)S(6)} %mul.184), channel_id=1, replica_groups=mesh['groups'=2,'dp'=4,'mp'=4] {'dp'}, use_global_device_ids=true, to_apply=%region_9.10 | all-reduce | flops 2 | bytes 16 | tf_op jit(solution)/shard_map/psum | solution.py:149
  (17 shorter events, 0.3 us)
Async XLA Ops:
  7.2 26.9 %copy-start = (bf16[2048,256]{1,0:T(8,128)(2,1)S(1)}, bf16[2048,256]{1,0:T(8,128)(2,1)}, u32[]{:S(2)}) copy-start(bf16[2048,256]{1,0:T(8,128)(2,1)} %param.16) | copy-start | bytes 3145732
  7.2 147.0 %all-reduce.6.cloned.1.call-start = ((), (), s32[]{:S(2)}) async-start(), calls=%async_computation.1 | async-start | bytes 258048
  29.3 4.9 %copy-start.1 = (bf16[2048,256]{1,0:T(8,128)(2,1)S(1)}, bf16[2048,256]{1,0:T(8,128)(2,1)}, u32[]{:S(2)}) copy-start(bf16[2048,256]{1,0:T(8,128)(2,1)} %param.15) | copy-start | bytes 3145732
  29.3 21.5 %copy-start.8 = (u32[32]{0:T(128)S(1)}, u32[32]{0:T(128)}, u32[]{:S(2)}) copy-start(u32[32]{0:T(128)} %constant.67) | copy-start | bytes 388
  29.3 24.6 %copy-start.2 = (bf16[1,2,256,128]{3,2,1,0:T(8,128)(2,1)S(1)}, bf16[1,2,256,128]{3,2,1,0:T(8,128)(2,1)}, u32[]{:S(2)}) copy-start(bf16[1,2,256,128]{3,2,1,0:T(8,128)(2,1)} %param.18) | copy-start | bytes 393220
  29.3 25.8 %copy-start.6 = (bf16[1,2,256,128]{3,2,1,0:T(8,128)(2,1)S(1)}, bf16[1,2,256,128]{3,2,1,0:T(8,128)(2,1)}, u32[]{:S(2)}) copy-start(bf16[1,2,256,128]{3,2,1,0:T(8,128)(2,1)} %param.19) | copy-start | bytes 393220
  34.5 48.8 %copy-start.7 = (u32[32]{0:T(128)S(1)}, u32[32]{0:T(128)}, u32[]{:S(2)}) copy-start(u32[32]{0:T(128)} %constant.71) | copy-start | bytes 388
  34.5 49.4 %copy-start.3 = (bf16[1,2048]{1,0:T(2,128)(2,1)S(1)}, bf16[1,2048]{1,0:T(2,128)(2,1)}, u32[]{:S(2)}) copy-start(bf16[1,2048]{1,0:T(2,128)(2,1)} %param.12) | copy-start | bytes 12292
  34.5 68.1 %copy-start.5 = (f32[8192]{0:T(1024)S(1)}, f32[8192]{0:T(1024)}, u32[]{:S(2)}) copy-start(f32[8192]{0:T(1024)} %param.21) | copy-start | bytes 98308
  84.6 40.5 %copy-start.4 = (bf16[1,2048]{1,0:T(2,128)(2,1)}, bf16[1,2048]{1,0:T(2,128)(2,1)S(1)}, u32[]{:S(2)}) copy-start(bf16[1,2048]{1,0:T(2,128)(2,1)S(1)} %fusion.21) | copy-start | bytes 12292
  84.6 5.5 %collective-permute-start = (bf16[1,2048]{1,0:T(2,128)(2,1)S(1)}, bf16[1,2048]{1,0:T(2,128)(2,1)S(1)}, u32[]{:S(2)}, u32[]{:S(2)}) collective-permute-start(bf16[1,2048]{1,0:T(2,128)(2,1)S(1)} %fusion.21), channel_id=1, source_target_pairs={{0,4},{4,8},{8,12},{12,0},{1,5},{5,9},{9,13},{13,1},{2,6},{6,10},{... | collective-permute-start | bytes 12296 | tf_op jit(solution)/shard_map/ppermute | solution.py:15
  90.1 5.4 %collective-permute-start.1 = (bf16[1,2048]{1,0:T(2,128)(2,1)S(1)}, bf16[1,2048]{1,0:T(2,128)(2,1)S(1)}, u32[]{:S(2)}, u32[]{:S(2)}) collective-permute-start(bf16[1,2048]{1,0:T(2,128)(2,1)S(1)} %collective-permute-done), channel_id=1, source_target_pairs={{0,4},{4,8},{8,12},{12,0},{1,5},{5,9},{9,13},{13,1},{2,6},{6,10},{... | collective-permute-start | bytes 12296 | tf_op jit(solution)/shard_map/ppermute | solution.py:15
  95.5 5.4 %collective-permute-start.2 = (bf16[1,2048]{1,0:T(2,128)(2,1)S(1)}, bf16[1,2048]{1,0:T(2,128)(2,1)S(1)}, u32[]{:S(2)}, u32[]{:S(2)}) collective-permute-start(bf16[1,2048]{1,0:T(2,128)(2,1)S(1)} %collective-permute-done.1), channel_id=1, source_target_pairs={{0,4},{4,8},{8,12},{12,0},{1,5},{5,9},{9,13},{13,1},{2,6},{6,10},{... | collective-permute-start | bytes 12296 | tf_op jit(solution)/shard_map/ppermute | solution.py:15
Sparse Core Ops, SparseCore 0:
  125.2 28.9 all-reduce.5
